TPU v7x, 32 devices: a whole 2x2x4 slice. The times are simulated.
32 devices in a mesh: groups: 2 (over y), seq: 4 (over z), fsdp: 2 (over x), sub: 2 (over core).
Axes of the slice: x: 2, y: 2, z: 4, core: 2. Of those that a mesh axis runs over, the one named last changes fastest.
Arguments:
- tokens: bfloat16 [2048, 8192], P(('groups', 'seq')), parts along dimension 0, may hold values from -400 to 400
- norm_gain: float32 [8192], replicated, may hold values from 0.1 to 1.9
- w_query: bfloat16 [8, 16, 8192], P(('seq', 'sub'), 'fsdp'), may hold values from -0.0625 to 0.0625
- w_key: bfloat16 [8, 16, 8192], P(('seq', 'sub'), 'fsdp'), may hold values from -0.0625 to 0.0625
- w_value: bfloat16 [8, 128, 8192], P(('seq', 'sub'), 'fsdp'), may hold values from -5 to 5
- head_gain: float32 [128], replicated, may hold values from 0.1 to 1.9
- w_out: bfloat16 [8, 128, 8192], P('seq', None, ('fsdp', 'sub')), may hold values from -0.1875 to 0.1875
Outputs:
- mixed: bfloat16 [2048, 8192], P(('groups', 'seq'), ('fsdp', 'sub')), parts along dimension 0
There are 2 independent parts, one for each index of `groups`. A program takes and returns all parts, laid end to end along the dimension named above; an argument that names none is the same for every part. Nothing has to cross between parts.
All inputs are finite; a program needn't handle non-finite values.
Results may differ from a plain program's by a relative error of at most 0.0084.
Values may be sent and summed in bfloat16 or wider, within the bound.
No kernel may reach another device: no remote copies, remote signals or barrier semaphores. Data moves between devices by JAX's collectives and lax.ppermute only.
A program may use at most 64 MiB of HBM per device.

v0:
```python
import math
import jax
import jax.numpy as jnp
import numpy as np
from jax import lax
from jax.sharding import PartitionSpec as P

BLOCK = 512


def taylor_first(vectors):
    feature_count = vectors.shape[0]
    first_row, second_row = np.triu_indices(feature_count, 1)
    cross_terms = vectors[first_row] * vectors[second_row] / 4.0
    squares = vectors * vectors / (4.0 * math.sqrt(2.0))
    leading = jnp.ones((1,) + vectors.shape[1:], jnp.float32)
    return jnp.concatenate([leading, vectors / 2.0, cross_terms, squares], 0)


def head_norm(numerator, head_gain, channel_axis):
    widened = numerator.astype(jnp.float32)
    meansq = jnp.mean(widened * widened, axis=channel_axis, keepdims=True)
    gain_shape = tuple((-1 if axis_pos == channel_axis else 1 for axis_pos in range(widened.ndim)))
    return (widened * lax.rsqrt(meansq + 1e-06) * head_gain.reshape(gain_shape)).astype(
        jnp.bfloat16
    )


def attend(queries, key_vectors, values_local):
    length = queries.shape[1]
    nblocks = length // BLOCK
    channels = values_local.shape[0]
    query_feats = taylor_first(queries.astype(jnp.float32)).astype(jnp.bfloat16)
    key_feats = taylor_first(key_vectors.astype(jnp.float32)).astype(jnp.bfloat16)
    taylor_width = query_feats.shape[0]
    contrib = jnp.einsum(
        "fbj,ebj->bfe",
        key_feats.reshape(taylor_width, nblocks, BLOCK),
        values_local.reshape(channels, nblocks, BLOCK),
        preferred_element_type=jnp.float32,
    )
    prefix = jnp.concatenate([jnp.zeros_like(contrib[:1]), jnp.cumsum(contrib[:-1], axis=0)], 0)
    prior_state = prefix.astype(jnp.bfloat16)
    carried = jnp.einsum(
        "bfe,fbt->bet",
        prior_state,
        query_feats.reshape(taylor_width, nblocks, BLOCK),
        preferred_element_type=jnp.float32,
    )
    earlier = lax.broadcasted_iota(jnp.int32, (BLOCK, BLOCK), 0)
    column_pos = lax.broadcasted_iota(jnp.int32, (BLOCK, BLOCK), 1)
    causal = earlier <= column_pos

    def one_block(block_index):
        offset = block_index * BLOCK
        query_block = lax.dynamic_slice_in_dim(queries, offset, BLOCK, 1)
        key_block = lax.dynamic_slice_in_dim(key_vectors, offset, BLOCK, 1)
        value_block = lax.dynamic_slice_in_dim(values_local, offset, BLOCK, 1)
        scores = jnp.einsum("fj,ft->jt", key_block, query_block, preferred_element_type=jnp.float32)
        kernel = 1.0 + scores / 4.0 + scores * scores / 32.0
        weight = jnp.where(causal, kernel, 0.0).astype(jnp.bfloat16)
        return jnp.einsum("ej,jt->et", value_block, weight, preferred_element_type=jnp.float32)

    local_part = lax.map(one_block, jnp.arange(nblocks, dtype=jnp.int32))
    numerator = (local_part + carried).astype(jnp.bfloat16)
    return jnp.transpose(numerator, (1, 0, 2)).reshape(channels, length)


def per_device(tokens, norm_gain, w_query, w_key, w_value, head_gain, w_out):
    feat_dev = w_query.shape[1]
    inputs = tokens.astype(jnp.float32)
    meansq = jnp.mean(inputs * inputs, axis=1, keepdims=True)
    normed = (inputs * lax.rsqrt(meansq + 1e-05) * norm_gain).astype(jnp.bfloat16)
    stacked = jnp.concatenate([w_query, w_key, w_value], 1)
    head_weights, out_weights = (
        lax.all_gather(stacked, "seq", axis=0, tiled=True),
        lax.all_gather(w_out, "seq", axis=0, tiled=True),
    )
    projected = jnp.einsum(
        "hcd,td->hct", head_weights, normed, preferred_element_type=jnp.float32
    ).astype(jnp.bfloat16)
    by_head = lax.all_to_all(projected, "seq", split_axis=0, concat_axis=2, tiled=True)
    qk_local = by_head[:, : 2 * feat_dev]
    values_local = by_head[0, 2 * feat_dev :]
    qk_whole = lax.all_gather(qk_local, "fsdp", axis=0, tiled=True)
    length = qk_whole.shape[2]
    queries = qk_whole[:, :feat_dev].reshape(-1, length)
    key_vectors = qk_whole[:, feat_dev:].reshape(-1, length)
    numerator = attend(queries, key_vectors, values_local)
    heads_total = out_weights.shape[0]
    head_width = out_weights.shape[1]
    by_token = lax.all_to_all(numerator[None], "seq", split_axis=2, concat_axis=0, tiled=True)
    everyone = lax.all_gather(by_token[None], ("fsdp", "sub"), axis=0, tiled=True)
    arranged = everyone.reshape(
        lax.axis_size("fsdp"),
        lax.axis_size("sub"),
        everyone.shape[1],
        everyone.shape[2],
        everyone.shape[3],
    )
    arranged = jnp.transpose(arranged, (2, 1, 0, 3, 4)).reshape(heads_total, head_width, -1)
    attended = head_norm(arranged, head_gain, 1)
    mixed = jnp.einsum("het,hed->td", attended, out_weights, preferred_element_type=jnp.float32)
    return mixed.astype(jnp.bfloat16)


def solution(mesh):
    in_specs = (
        P(("groups", "seq"), None),
        P(),
        P(("seq", "sub"), "fsdp", None),
        P(("seq", "sub"), "fsdp", None),
        P(("seq", "sub"), "fsdp", None),
        P(),
        P("seq", None, ("fsdp", "sub")),
    )
    out_specs = P(("groups", "seq"), ("fsdp", "sub"))
    return jax.shard_map(
        per_device, mesh=mesh, in_specs=in_specs, out_specs=out_specs, check_vma=False
    )
```

profile of v0, /device:TPU:0, one launch (start us, length us, event | category | flops | bytes accessed | tf_op | source)
XLA Modules:
  0.0 208.2 jit_solution(16304550115294808762)
XLA Ops:
  6.5 0.0 copy-start.2
  6.5 0.0 all-gather.4.cloned.1.call-start
  6.5 2.5 %pad_maximum_fusion = bf16[1,80,8192]{2,1,0:T(8,128)(2,1)} fusion(bf16[1,64,8192]{2,1,0:T(8,128)(2,1)} %param.21, bf16[1,8,8192]{2,1,0:T(8,128)(2,1)} %param.20, bf16[1,8,8192]{2,1,0:T(8,128)(2,1)} %param.19), kind=kLoop, calls=%fused_computation.32 | loop fusion | flops 3932160 | bytes 2621440 | tf_op jit(solution)/shard_map/concatenate | solution.py:74
  9.0 0.0 all-gather.4.cloned.1.call-update
  9.0 0.0 all-gather.6.cloned.1.call-start
  9.1 0.7 all-gather.6.cloned.1.call-update
  9.8 3.1 %fusion.18 = f32[256]{0:T(256)S(1)} fusion(bf16[256,8192]{1,0:T(8,128)(2,1)} %param.17), kind=kLoop, calls=%fused_computation.23 | loop fusion | flops 6291200 | bytes 4195328 | tf_op jit(solution)/shard_map/reduce_sum | solution.py:72
  12.9 0.0 copy-start.1
  12.9 0.0 copy-start
  12.9 97.0 %all-gather.4.cloned.1.call-done = bf16[4,80,8192]{2,1,0:T(8,128)(2,1)} async-done(((bf16[1,80,8192]{2,1,0:T(8,128)(2,1)}), bf16[4,80,8192]{2,1,0:T(8,128)(2,1)}) %all-gather.4.cloned.1.call-update) | async-done | bytes 5242896 | tf_op jit(solution)/shard_map/all_gather | solution.py:76
  110.0 0.0 copy-done.2
  110.0 6.1 %fusion.27 = bf16[4,80,256]{2,1,0:T(8,128)(2,1)} fusion(bf16[4,80,8192]{2,1,0:T(8,128)(2,1)} %all-gather.4.cloned.1.call-done, bf16[256,8192]{1,0:T(8,128)(2,1)} %param.17, f32[8192]{0:T(1024)S(1)} %copy-done.2, f32[256]{0:T(256)S(1)} %add_rsqrt_fusion), kind=kOutput, calls=%fused_computation.34 | convolution fusion | flops 1350647808 | bytes 9634816 | tf_op jit(solution)/shard_map/hcd,td->hct/dot_general | solution.py:79
  116.0 3.3 %all-to-all-start = ((bf16[4,80,256]{2,1,0:T(8,128)(2,1)}), bf16[4,80,256]{2,1,0:T(8,128)(2,1)S(1)}, u32[]{:S(2)}, u32[]{:S(2)}) async-start(bf16[4,80,256]{2,1,0:T(8,128)(2,1)} %fusion.27), calls=%async_computation | async-start | bytes 327680 | tf_op jit(solution)/shard_map/all_to_all | solution.py:82
  119.4 0.0 copy-done.1
  119.4 0.0 copy-done
  119.5 11.4 %all-to-all-done = bf16[4,80,256]{2,1,0:T(8,128)(2,1)S(1)} async-done(((bf16[4,80,256]{2,1,0:T(8,128)(2,1)}), bf16[4,80,256]{2,1,0:T(8,128)(2,1)S(1)}, u32[]{:S(2)}, u32[]{:S(2)}) %all-to-all-start) | async-done | bytes 163872 | tf_op jit(solution)/shard_map/all_to_all | solution.py:82
  130.9 4.6 %all_gather.13 = bf16[2,16,1024]{2,1,0:T(8,128)(2,1)S(1)} all-gather(bf16[1,16,1024]{2,1,0:T(8,128)(2,1)S(1)} %slice.30), channel_id=1, replica_groups=mesh['groups'=2,'seq'=4,'fsdp'=2,'sub'=2] {'fsdp'}, dimensions={0}, use_global_device_ids=true | all-gather | bytes 98304 | tf_op jit(solution)/shard_map/all_gather | solution.py:85
  135.5 0.8 gather_fusion
  136.3 0.8 gather_fusion.1
  137.1 0.8 gather_fusion.2
  137.9 0.8 gather_fusion.3
  138.7 0.1 multiply_convert_fusion.3
  138.9 0.1 reshape_squeeze.3
  139.0 0.1 multiply_convert_fusion.2
  139.2 0.3 fusion.34
  139.5 3.5 %while.11 = (s32[]{:T(128)}, f32[2,64,512]{2,1,0:T(8,128)S(1)}, s32[2]{0:T(128)S(1)}, bf16[64,1024]{1,0:T(8,128)(2,1)S(1)}, bf16[16,1024]{1,0:T(8,128)(2,1)S(1)}...) while((s32[]{:T(128)}, f32[2,64,512]{2,1,0:T(8,128)S(1)}, ...), condition=%wide.region_2.3_spmd.clone, body=%wide.region_1.0_spmd.clone.sunk | while | flops 44040196 | bytes 231075 | solution.py:64
  139.5 0.6 dynamic_slice.32
  140.7 0.5 fusion.70
  141.2 0.6 dynamic_slice.32
  142.5 0.5 fusion.70
  142.9 0.3 fusion.31
  143.2 0.2 copy.83
  143.4 0.1 reshape.135
  143.6 0.0 copy-start.3
  143.6 0.5 broadcast.135
  144.1 2.3 %reduce.7 = bf16[1024,64]{1,0:T(8,128)(2,1)S(1)} reduce(bf16[1024,1,64]{2,1,0:T(2,128)(2,1)S(1)} %bitcast.63, bf16[]{:T(256)} %broadcast.135), dimensions={1}, to_apply=%bitcast.51.reduce_sub_computation | reduce | bytes 262146
  146.4 0.2 reshape.137
  146.6 13.8 %all_to_all.33 = bf16[4,2,8192]{2,1,0:T(2,128)(2,1)S(1)} all-to-all(bf16[4,2,8192]{2,1,0:T(2,128)(2,1)S(1)} %reshape.137), channel_id=1, replica_groups=mesh['groups'=2,'seq'=4,'fsdp'=2,'sub'=2] {'seq'}, dimensions={0} | all-to-all | bytes 262144 | tf_op jit(solution)/shard_map/all_to_all | solution.py:92
  160.4 0.3 reshape.138
  160.8 0.3 copy.76
  161.1 0.1 all_to_all.29
  161.2 7.1 %all-gather = bf16[16,1,64,256]{3,2,1,0:T(8,128)(2,1)S(1)} all-gather(bf16[4,1,64,256]{3,2,1,0:T(8,128)(2,1)S(1)} %copy.77), channel_id=2, replica_groups=mesh['groups'=2,'seq'=4,'fsdp'=2,'sub'=2] {'fsdp','sub'}, dimensions={0}, use_global_device_ids=true | all-gather | bytes 655360 | tf_op jit(solution)/shard_map/all_gather | solution.py:93
  168.3 0.1 bitcast_convert_fusion
  168.5 0.1 copy.79
  168.6 0.1 multiply_reduce_fusion
  168.8 28.0 %all-gather.6.cloned.1.call-done = bf16[8,128,2048]{2,1,0:T(8,128)(2,1)} async-done(((bf16[2,128,2048]{2,1,0:T(8,128)(2,1)}), bf16[8,128,2048]{2,1,0:T(8,128)(2,1)}) %all-gather.6.cloned.1.call-update) | async-done | bytes 4194320 | tf_op jit(solution)/shard_map/all_gather | solution.py:77
  196.8 0.0 copy-done.3
  196.8 4.5 %fusion.26 = bf16[256,2048]{1,0:T(8,128)(2,1)} fusion(bf16[8,128,2048]{2,1,0:T(8,128)(2,1)} %all-gather.6.cloned.1.call-done, f32[8,128,256]{2,1,0:T(8,128)S(1)} %bitcast.64, f32[128]{0:T(128)S(1)} %copy-done.3, f32[8,256]{1,0:T(8,128)S(1)} %rsqrt.21), kind=kOutput, calls=%fused_computation.31 | convolution fusion | flops 1075052544 | bytes 6300160 | tf_op jit(solution)/shard_map/het,hed->td/dot_general | solution.py:103
  (27 shorter events, 0.3 us)
Async XLA Ops:
  6.5 103.4 %copy-start.2 = (f32[8192]{0:T(1024)S(1)}, f32[8192]{0:T(1024)}, u32[]{:S(2)}) copy-start(f32[8192]{0:T(1024)} %param.18) | copy-start | bytes 98308
  6.5 103.4 %all-gather.4.cloned.1.call-start = ((), (), s32[]{:S(2)}) async-start(), calls=%async_computation.2 | async-start | bytes 6553600 | tf_op jit(solution)/shard_map/all_gather | solution.py:76
  9.0 187.8 %all-gather.6.cloned.1.call-start = ((), (), s32[]{:S(2)}) async-start(), calls=%async_computation.3 | async-start | bytes 5242880 | tf_op jit(solution)/shard_map/all_gather | solution.py:77
  12.9 106.5 %copy-start.1 = (s32[120]{0:T(128)S(1)}, s32[120]{0:T(128)}, u32[]{:S(2)}) copy-start(s32[120]{0:T(128)} %constant.78) | copy-start | bytes 1444
  12.9 106.5 %copy-start = (s32[120]{0:T(128)S(1)}, s32[120]{0:T(128)}, u32[]{:S(2)}) copy-start(s32[120]{0:T(128)} %constant.79) | copy-start | bytes 1444
  116.0 14.8 %all-to-all-start = ((bf16[4,80,256]{2,1,0:T(8,128)(2,1)}), bf16[4,80,256]{2,1,0:T(8,128)(2,1)S(1)}, u32[]{:S(2)}, u32[]{:S(2)}) async-start(bf16[4,80,256]{2,1,0:T(8,128)(2,1)} %fusion.27), calls=%async_computation | async-start | bytes 327680 | tf_op jit(solution)/shard_map/all_to_all | solution.py:82
  143.6 53.3 %copy-start.3 = (f32[128]{0:T(128)S(1)}, f32[128]{0:T(128)}, u32[]{:S(2)}) copy-start(f32[128]{0:T(128)} %param.22) | copy-start | bytes 1540
Sparse Core Ops, SparseCore 0:
  9.2 100.7 all-gather.3
  111.5 85.2 all-gather.5
where the time goes:
time: 209 us; the launch traced here: 208 us
  waiting for transfers between devices  137 us (66%)
  blocking collectives  25.6 us (12%)
  between operations  13.8 us (7%)
  matrix products  12.1 us (6%)
  other arithmetic  8.29 us (4%)
  local copies, waits for them, and re-layouts  6.51 us (3%)
  starting transfers between devices  3.39 us (2%)
    all_gather x1, waiting for transfers between devices, per_device(): lax.all_gather(stacked, 'seq', axis=0, tiled=True)  97 us
    all_gather x1, waiting for transfers between devices, per_device(): lax.all_gather(w_out, 'seq', axis=0, tiled=True)  28 us
    all_to_all x1, blocking collectives, per_device(): lax.all_to_all(numerator[None], 'seq', split_axis=2, concat_axis=0, tiled...  13.8 us
    all_to_all x1, waiting for transfers between devices, per_device(): lax.all_to_all(projected, 'seq', split_axis=0, concat_axis=2, tiled=True)  11.4 us
    all_gather x1, blocking collectives, per_device(): lax.all_gather(by_token[None], ('fsdp', 'sub'), axis=0, tiled=True)  7.15 us
    dot_general x1, matrix products, per_device(): jnp.einsum('hcd,td->hct', head_weights, normed, preferred_element_type=jn...  6.07 us
    all_gather x1, blocking collectives, per_device(): qk_whole = lax.all_gather(qk_local, 'fsdp', axis=0, tiled=True)  4.58 us
    dot_general x1, matrix products, per_device(): jnp.einsum('het,hed->td', attended, out_weights, preferred_element_type=j...  4.52 us
  transfers between devices with their start and end apart: 3, of which 3 were waited for; matrix products, arithmetic and copies ran while one was open for 10% of the time, Pallas kernels for 0%

commit v1 on v0

--- a/solution.py
+++ b/solution.py
@@ -79,7 +79,19 @@
     projected = jnp.einsum(
         "hcd,td->hct", head_weights, normed, preferred_element_type=jnp.float32
     ).astype(jnp.bfloat16)
-    by_head = lax.all_to_all(projected, "seq", split_axis=0, concat_axis=2, tiled=True)
+    ways, here = (lax.axis_size("seq"), lax.axis_index("seq"))
+    width = projected.shape[0] // ways
+    shape = list(projected.shape)
+    shape[0] = width
+    height = shape[2]
+    shape[2] = height * ways
+    full = jnp.zeros(shape, projected.dtype)
+    for mask in range(ways):
+        part = lax.dynamic_slice_in_dim(projected, (here ^ mask) * width, width, axis=0)
+        if mask:
+            part = lax.ppermute(part, "seq", [(d, d ^ mask) for d in range(ways)])
+        full = lax.dynamic_update_slice_in_dim(full, part, (here ^ mask) * height, axis=2)
+    by_head = full
     qk_local = by_head[:, : 2 * feat_dev]
     values_local = by_head[0, 2 * feat_dev :]
     qk_whole = lax.all_gather(qk_local, "fsdp", axis=0, tiled=True)

time: 209 us -> 205 us (0.981)
  waiting for transfers between devices: 137 us -> 133 us
    all_to_all x1 -> x0, waiting for transfers between devices: 11.4 us -> none  [per_device(): lax.all_to_all(projected, 'seq', split_axis=0, concat_axis=2, tiled=True)]
    all_gather x1, waiting for transfers between devices: 28 us -> 33.2 us  [per_device(): lax.all_gather(w_out, 'seq', axis=0, tiled=True)]
    ppermute x0 -> x3, starting transfers between devices: none -> 4.5 us  [per_device(): part = lax.ppermute(part, 'seq', [(d, d ^ mask) for d in range(ways)])]
    all_to_all x1 -> x0, starting transfers between devices: 3.35 us -> none  [per_device(): lax.all_to_all(projected, 'seq', split_axis=0, concat_axis=2, tiled=True)]
    ppermute x0 -> x3, waiting for transfers between devices: none -> 2.51 us  [per_device(): part = lax.ppermute(part, 'seq', [(d, d ^ mask) for d in range(ways)])]
  transfers between devices with their start and end apart: 3 -> 5, of which waited for: 3 -> 4; matrix products, arithmetic and copies ran while one was open for 10% -> 9% of each run, Pallas kernels for 0% -> 0%
where the time goes in v1:
time: 205 us
  waiting for transfers between devices  133 us (65%)
  blocking collectives  25.4 us (12%)
  between operations  13.8 us (7%)
  matrix products  11.4 us (6%)
  other arithmetic  8.29 us (4%)
  local copies, waits for them, and re-layouts  6.71 us (3%)
  starting transfers between devices  4.54 us (2%)
    all_gather x1, waiting for transfers between devices, per_device(): lax.all_gather(stacked, 'seq', axis=0, tiled=True)  97 us
    all_gather x1, waiting for transfers between devices, per_device(): lax.all_gather(w_out, 'seq', axis=0, tiled=True)  33.2 us
    all_to_all x1, blocking collectives, per_device(): lax.all_to_all(numerator[None], 'seq', split_axis=2, concat_axis=0, tiled...  13.5 us
    all_gather x1, blocking collectives, per_device(): lax.all_gather(by_token[None], ('fsdp', 'sub'), axis=0, tiled=True)  7.22 us
    dot_general x1, matrix products, per_device(): jnp.einsum('hcd,td->hct', head_weights, normed, preferred_element_type=jn...  5.4 us
    all_gather x1, blocking collectives, per_device(): qk_whole = lax.all_gather(qk_local, 'fsdp', axis=0, tiled=True)  4.58 us
    dot_general x1, matrix products, per_device(): jnp.einsum('het,hed->td', attended, out_weights, preferred_element_type=j...  4.51 us
    ppermute x3, starting transfers between devices, per_device(): part = lax.ppermute(part, 'seq', [(d, d ^ mask) for d in range(ways)])  4.5 us
  transfers between devices with their start and end apart: 5, of which 4 were waited for; matrix products, arithmetic and copies ran while one was open for 9% of the time, Pallas kernels for 0%

profile of v1, /device:TPU:0, one launch (start us, length us, event | category | flops | bytes accessed | tf_op | source)
XLA Modules:
  0.0 205.1 jit_solution(9594289442078932371)
XLA Ops:
  6.5 0.0 all-gather.4.cloned.1.call-start
  6.5 2.5 %pad_maximum_fusion = bf16[1,80,8192]{2,1,0:T(8,128)(2,1)} fusion(bf16[1,64,8192]{2,1,0:T(8,128)(2,1)} %param.21, bf16[1,8,8192]{2,1,0:T(8,128)(2,1)} %param.20, bf16[1,8,8192]{2,1,0:T(8,128)(2,1)} %param.19), kind=kLoop, calls=%fused_computation.32 | loop fusion | flops 3932160 | bytes 2621440 | tf_op jit(solution)/shard_map/concatenate | solution.py:74
  9.0 0.0 all-gather.4.cloned.1.call-update
  9.0 0.0 all-gather.6.cloned.1.call-start
  9.1 0.7 all-gather.6.cloned.1.call-update
  9.8 0.0 copy-done.1
  9.8 3.1 %fusion.18 = f32[256]{0:T(256)S(1)} fusion(bf16[256,8192]{1,0:T(8,128)(2,1)} %param.17), kind=kLoop, calls=%fused_computation.23 | loop fusion | flops 6291200 | bytes 4195328 | tf_op jit(solution)/shard_map/reduce_sum | solution.py:72
  13.0 97.0 %all-gather.4.cloned.1.call-done = bf16[4,80,8192]{2,1,0:T(8,128)(2,1)} async-done(((bf16[1,80,8192]{2,1,0:T(8,128)(2,1)}), bf16[4,80,8192]{2,1,0:T(8,128)(2,1)}) %all-gather.4.cloned.1.call-update) | async-done | bytes 5242896 | tf_op jit(solution)/shard_map/all_gather | solution.py:76
  110.0 0.0 copy-done.2
  110.0 5.4 %fusion.27 = bf16[4,80,256]{2,1,0:T(8,128)(2,1)S(1)} fusion(bf16[4,80,8192]{2,1,0:T(8,128)(2,1)} %all-gather.4.cloned.1.call-done, bf16[256,8192]{1,0:T(8,128)(2,1)} %param.17, f32[8192]{0:T(1024)S(1)} %copy-done.2, f32[256]{0:T(256)S(1)} %add_rsqrt_fusion), kind=kOutput, calls=%fused_computation.34 | convolution fusion | flops 1350647808 | bytes 9634816 | tf_op jit(solution)/shard_map/hcd,td->hct/dot_general | solution.py:79
  115.4 0.1 collective-permute-start
  115.5 0.0 copy-done
  115.6 1.0 collective-permute-start.1
  116.6 3.4 %collective-permute-start.2 = (bf16[1,80,256]{2,1,0:T(8,128)(2,1)S(1)}, bf16[1,80,256]{2,1,0:T(8,128)(2,1)S(1)}, u32[]{:S(2)}, u32[]{:S(2)}) collective-permute-start(bf16[1,80,256]{2,1,0:T(8,128)(2,1)S(1)} %get-tuple-element.71), channel_id=1, source_target_pairs={{0,12},{4,8},{8,4},{12,0},{1,13},{5,9},{9,5},{13,1},{2,14},{6,10},... | collective-permute-start | bytes 122888 | tf_op jit(solution)/shard_map/ppermute | solution.py:92
  120.0 0.0 collective-permute-done
  120.0 1.5 collective-permute-done.1
  121.5 1.0 collective-permute-done.2
  122.6 4.6 %all_gather.13 = bf16[2,16,1024]{2,1,0:T(8,128)(2,1)S(1)} all-gather(bf16[1,16,1024]{2,1,0:T(8,128)(2,1)S(1)} %slice.30), channel_id=1, replica_groups=mesh['groups'=2,'seq'=4,'fsdp'=2,'sub'=2] {'fsdp'}, dimensions={0}, use_global_device_ids=true | all-gather | bytes 98304 | tf_op jit(solution)/shard_map/all_gather | solution.py:97
  127.2 0.8 gather_fusion
  127.9 0.8 gather_fusion.1
  128.7 0.8 gather_fusion.2
  129.5 0.8 gather_fusion.3
  130.3 0.1 multiply_convert_fusion.3
  130.4 0.1 reshape_squeeze.3
  130.6 0.1 multiply_convert_fusion.2
  130.8 0.3 fusion.34
  131.1 3.7 %while.11 = (s32[]{:T(128)}, f32[2,64,512]{2,1,0:T(8,128)S(1)}, s32[2]{0:T(128)S(1)}, bf16[64,1024]{1,0:T(8,128)(2,1)S(1)}, bf16[16,1024]{1,0:T(8,128)(2,1)S(1)}...) while((s32[]{:T(128)}, f32[2,64,512]{2,1,0:T(8,128)S(1)}, ...), condition=%wide.region_2.3_spmd.clone, body=%wide.region_1.0_spmd.clone.sunk | while | flops 44040196 | bytes 231075 | solution.py:64
  131.2 0.7 dynamic_slice.52
  132.5 0.5 fusion.70
  133.0 0.7 dynamic_slice.52
  134.4 0.5 fusion.70
  134.9 0.3 fusion.31
  135.1 0.2 copy.78
  135.3 0.1 reshape.135
  135.5 0.0 copy-start.3
  135.5 0.5 broadcast.135
  136.0 2.3 %reduce.7 = bf16[1024,64]{1,0:T(8,128)(2,1)S(1)} reduce(bf16[1024,1,64]{2,1,0:T(2,128)(2,1)S(1)} %bitcast.58, bf16[]{:T(256)} %broadcast.135), dimensions={1}, to_apply=%bitcast.46.reduce_sub_computation | reduce | bytes 262146
  138.3 0.2 reshape.137
  138.5 13.5 %all_to_all.15 = bf16[4,2,8192]{2,1,0:T(2,128)(2,1)S(1)} all-to-all(bf16[4,2,8192]{2,1,0:T(2,128)(2,1)S(1)} %reshape.137), channel_id=1, replica_groups=mesh['groups'=2,'seq'=4,'fsdp'=2,'sub'=2] {'seq'}, dimensions={0} | all-to-all | bytes 262144 | tf_op jit(solution)/shard_map/all_to_all | solution.py:104
  152.1 0.3 reshape.138
  152.4 0.3 copy.71
  152.7 0.1 all_to_all.12
  152.8 7.2 %all-gather = bf16[16,1,64,256]{3,2,1,0:T(8,128)(2,1)S(1)} all-gather(bf16[4,1,64,256]{3,2,1,0:T(8,128)(2,1)S(1)} %copy.72), channel_id=2, replica_groups=mesh['groups'=2,'seq'=4,'fsdp'=2,'sub'=2] {'fsdp','sub'}, dimensions={0}, use_global_device_ids=true | all-gather | bytes 655360 | tf_op jit(solution)/shard_map/all_gather | solution.py:105
  160.0 0.1 bitcast_convert_fusion
  160.2 0.1 copy.74
  160.3 0.1 multiply_reduce_fusion
  160.5 33.2 %all-gather.6.cloned.1.call-done = bf16[8,128,2048]{2,1,0:T(8,128)(2,1)} async-done(((bf16[2,128,2048]{2,1,0:T(8,128)(2,1)}), bf16[8,128,2048]{2,1,0:T(8,128)(2,1)}) %all-gather.6.cloned.1.call-update) | async-done | bytes 4194320 | tf_op jit(solution)/shard_map/all_gather | solution.py:77
  193.7 4.5 %fusion.26 = bf16[256,2048]{1,0:T(8,128)(2,1)} fusion(bf16[8,128,2048]{2,1,0:T(8,128)(2,1)} %all-gather.6.cloned.1.call-done, f32[8,128,256]{2,1,0:T(8,128)S(1)} %bitcast.59, f32[128]{0:T(128)S(1)} %copy-done.3, f32[8,256]{1,0:T(8,128)S(1)} %rsqrt.21), kind=kOutput, calls=%fused_computation.31 | convolution fusion | flops 1075052544 | bytes 6300160 | tf_op jit(solution)/shard_map/het,hed->td/dot_general | solution.py:115
  (35 shorter events, 0.4 us)
Async XLA Ops:
  6.5 3.3 %copy-start.1 = (s32[120]{0:T(128)S(1)}, s32[120]{0:T(128)}, u32[]{:S(2)}) copy-start(s32[120]{0:T(128)} %constant.96) | copy-start | bytes 1444
  6.5 103.4 %copy-start.2 = (f32[8192]{0:T(1024)S(1)}, f32[8192]{0:T(1024)}, u32[]{:S(2)}) copy-start(f32[8192]{0:T(1024)} %param.18) | copy-start | bytes 98308
  6.5 103.4 %all-gather.4.cloned.1.call-start = ((), (), s32[]{:S(2)}) async-start(), calls=%async_computation.1 | async-start | bytes 6553600 | tf_op jit(solution)/shard_map/all_gather | solution.py:76
  9.0 184.7 %all-gather.6.cloned.1.call-start = ((), (), s32[]{:S(2)}) async-start(), calls=%async_computation.2 | async-start | bytes 5242880 | tf_op jit(solution)/shard_map/all_gather | solution.py:77
  13.0 102.6 %copy-start = (s32[120]{0:T(128)S(1)}, s32[120]{0:T(128)}, u32[]{:S(2)}) copy-start(s32[120]{0:T(128)} %constant.97) | copy-start | bytes 1444
  115.4 4.6 %collective-permute-start = (bf16[1,80,256]{2,1,0:T(8,128)(2,1)S(1)}, bf16[1,80,256]{2,1,0:T(8,128)(2,1)S(1)}, u32[]{:S(2)}, u32[]{:S(2)}) collective-permute-start(bf16[1,80,256]{2,1,0:T(8,128)(2,1)S(1)} %get-tuple-element.73), channel_id=1, source_target_pairs={{0,4},{4,0},{8,12},{12,8},{1,5},{5,1},{9,13},{13,9},{2,6},{6,2},{1... | collective-permute-start | bytes 122888 | tf_op jit(solution)/shard_map/ppermute | solution.py:92
  115.6 5.9 %collective-permute-start.1 = (bf16[1,80,256]{2,1,0:T(8,128)(2,1)S(1)}, bf16[1,80,256]{2,1,0:T(8,128)(2,1)S(1)}, u32[]{:S(2)}, u32[]{:S(2)}) collective-permute-start(bf16[1,80,256]{2,1,0:T(8,128)(2,1)S(1)} %get-tuple-element.72), channel_id=1, source_target_pairs={{0,8},{4,12},{8,0},{12,4},{1,9},{5,13},{9,1},{13,5},{2,10},{6,14},... | collective-permute-start | bytes 122888 | tf_op jit(solution)/shard_map/ppermute | solution.py:92
  116.6 5.9 %collective-permute-start.2 = (bf16[1,80,256]{2,1,0:T(8,128)(2,1)S(1)}, bf16[1,80,256]{2,1,0:T(8,128)(2,1)S(1)}, u32[]{:S(2)}, u32[]{:S(2)}) collective-permute-start(bf16[1,80,256]{2,1,0:T(8,128)(2,1)S(1)} %get-tuple-element.71), channel_id=1, source_target_pairs={{0,12},{4,8},{8,4},{12,0},{1,13},{5,9},{9,5},{13,1},{2,14},{6,10},... | collective-permute-start | bytes 122888 | tf_op jit(solution)/shard_map/ppermute | solution.py:92
  135.5 58.3 %copy-start.3 = (f32[128]{0:T(128)S(1)}, f32[128]{0:T(128)}, u32[]{:S(2)}) copy-start(f32[128]{0:T(128)} %param.22) | copy-start | bytes 1540
Sparse Core Ops, SparseCore 0:
  9.2 100.7 all-gather.3
  111.5 82.1 all-gather.5
